TPU v7x, 32 devices: a whole 2x2x4 slice. The times are simulated.
32 devices in a mesh: vocab: 8 (over y, x, core), seq: 4 (over z).
Axes of the slice: x: 2, y: 2, z: 4, core: 2. Of those that a mesh axis runs over, the one named last changes fastest.
Arguments:
- latent_vector: bfloat16 [32, 7168], P('vocab', 'seq'), may hold values from -400 to 400
- unembedding_matrix: bfloat16 [7168, 8192], P('seq', 'vocab'), may hold values from -0.0625 to 0.0625
- occurrence_tally: int32 [32, 8192], P(('seq', 'vocab')), may hold values from 0 to 2
- additive_offset_table: bfloat16 [32, 8192], P(('seq', 'vocab')), may hold values from 0 to 0.5
- recurrence_charge: float32 [32], P(('seq', 'vocab')), may hold values from 0.05 to 0.5
- appearance_charge: float32 [32], P(('seq', 'vocab')), may hold values from 0.6 to 1.5
- recurrence_divisor: float32 [32], P('seq'), may hold values from 1.05 to 1.6
- softening_divisor: float32 [32], P('seq'), may hold values from 0.5 to 1.5
- nucleus_share_limit: float32 [32], P('seq'), may hold values from 0.5 to 0.95
Outputs:
- penalized_logits: bfloat16 [32, 8192], P('seq', 'vocab')
- cutoff: float32 [32], P('seq')
Inputs may be any that keep to these rules, and one draw needn't show every extreme that they name: `appearance_charge`: each sequence's presence penalty exceeds every entry of its token bias.
All inputs are finite; a program needn't handle non-finite values.
Results may differ from a plain program's by a relative error of at most 0.0047.
Values may be sent and summed in bfloat16 or wider, within the bound.
No kernel may reach another device: no remote copies, remote signals or barrier semaphores. Data moves between devices by JAX's collectives and lax.ppermute only.
A program may use at most 64 MiB of HBM per device.

v0:
```python
import jax
import jax.numpy as jnp
from jax import lax
from jax.sharding import PartitionSpec as P

STEPS = 9


cutoff_span = 32.0


def per_device(
    latent_vector,
    unembedding_matrix,
    occurrence_tally,
    additive_offset_table,
    recurrence_charge,
    appearance_charge,
    recurrence_divisor,
    softening_divisor,
    nucleus_share_limit,
):
    count_float = occurrence_tally.astype(jnp.float32)
    offset = (
        additive_offset_table.astype(jnp.float32)
        - recurrence_charge[:, None] * count_float
        - appearance_charge[:, None] * (occurrence_tally > 0).astype(jnp.float32)
    ).astype(jnp.bfloat16)
    relaid = lax.all_to_all(offset, "vocab", split_axis=1, concat_axis=0, tiled=True)
    partial_logits = jnp.dot(
        lax.all_gather(latent_vector, "vocab", axis=0, tiled=True),
        unembedding_matrix,
        preferred_element_type=jnp.float32,
    )
    logits = lax.psum_scatter(partial_logits, "seq", scatter_dimension=0, tiled=True)
    seen_mask = relaid < 0
    factor = recurrence_divisor[:, None]
    discouraged_scores = jnp.where(
        seen_mask, jnp.where(logits > 0, logits / factor, logits * factor), logits
    ) + relaid.astype(jnp.float32)
    softened_scores = discouraged_scores / softening_divisor[:, None]
    largest_score = lax.pmax(jnp.max(softened_scores, axis=1), "vocab")
    exponential_values = jnp.exp(softened_scores - largest_score[:, None])
    row_total = lax.psum(jnp.sum(exponential_values, axis=1), "vocab")
    target = nucleus_share_limit * row_total
    start_bounds = (jnp.zeros_like(largest_score), jnp.ones_like(largest_score))
    fractions = jnp.arange(1, 8, dtype=jnp.float32)

    def refine(turn_index, bounds):
        lower_end, upper_end = bounds
        stride = (upper_end - lower_end) * 0.125
        probes = lower_end[:, None] + stride[:, None] * fractions[None, :]
        threshold_candidates = largest_score[:, None] - cutoff_span * probes
        inside = softened_scores[:, None, :] >= threshold_candidates[:, :, None]
        partial_mass = jnp.sum(jnp.where(inside, exponential_values[:, None, :], 0.0), axis=2)
        cumulative_shares = lax.psum(partial_mass, "vocab")
        below_count = jnp.sum((cumulative_shares < target[:, None]).astype(jnp.float32), axis=1)
        new_lower = lower_end + stride * below_count
        return (new_lower, new_lower + stride)

    lower_end, upper_end = lax.fori_loop(0, STEPS // 3, refine, start_bounds)
    return (discouraged_scores.astype(jnp.bfloat16), largest_score - cutoff_span * upper_end)


def solution(mesh):
    in_specs = (
        P("vocab", "seq"),
        P("seq", "vocab"),
        P(("seq", "vocab"), None),
        P(("seq", "vocab"), None),
        P(("seq", "vocab")),
        P(("seq", "vocab")),
        P("seq"),
        P("seq"),
        P("seq"),
    )
    out_specs = (P("seq", "vocab"), P("seq"))
    return jax.shard_map(
        per_device, mesh=mesh, in_specs=in_specs, out_specs=out_specs, check_vma=False
    )
```

profile of v0, /device:TPU:0, one launch (start us, length us, event | category | flops | bytes accessed | tf_op | source)
XLA Modules:
  0.0 110.7 jit_solution(10906374789269794412)
XLA Ops:
  7.2 0.0 copy-start
  7.2 0.0 copy-start.1
  7.2 0.0 copy-start.3
  7.2 0.0 copy-start.2
  7.2 0.0 copy-start.4
  7.2 0.0 reduce-scatter.2.cloned.1.call-start
  7.3 10.9 %all-gather = bf16[8,4,1792]{2,1,0:T(4,128)(2,1)S(1)} all-gather(bf16[1,4,1792]{2,1,0:T(4,128)(2,1)} %bitcast.19), channel_id=1, replica_groups=mesh['vocab'=8,'seq'=4] {'vocab'}, dimensions={0}, use_global_device_ids=true | all-gather | bytes 129024 | tf_op jit(solution)/shard_map/all_gather | solution.py:31
  18.2 3.4 %fusion.9 = f32[32,1024]{1,0:T(8,128)} fusion(bf16[32,1792]{1,0:T(8,128)(2,1)S(1)} %reshape.88, bf16[1792,1024]{1,0:T(8,128)(2,1)} %param.12), kind=kOutput, calls=%fused_computation.20 | convolution fusion | flops 117440512 | bytes 3915776 | tf_op jit(solution)/shard_map/dot_general | solution.py:30
  21.6 0.0 reduce-scatter.2.cloned.1.call-update
  22.9 0.0 copy-done
  23.0 0.0 copy-done.1
  23.0 0.1 fusion.5
  23.0 0.5 broadcast.112
  23.6 0.7 reduce
  24.3 0.6 reshape.89
  24.9 3.3 %all-to-all-start = ((bf16[8,2,512]{2,1,0:T(2,128)(2,1)}), bf16[8,2,512]{2,1,0:T(2,128)(2,1)S(1)}, u32[]{:S(2)}, u32[]{:S(2)}) async-start(bf16[8,2,512]{2,1,0:T(2,128)(2,1)} %reshape.89), calls=%async_computation | async-start | bytes 32768 | tf_op jit(solution)/shard_map/all_to_all | solution.py:29
  28.3 4.7 %all-to-all-done = bf16[8,2,512]{2,1,0:T(2,128)(2,1)S(1)} async-done(((bf16[8,2,512]{2,1,0:T(2,128)(2,1)}), bf16[8,2,512]{2,1,0:T(2,128)(2,1)S(1)}, u32[]{:S(2)}, u32[]{:S(2)}) %all-to-all-start) | async-done | bytes 16416 | tf_op jit(solution)/shard_map/all_to_all | solution.py:29
  33.0 8.5 %reduce-scatter.2.cloned.1.call-done = f32[8,1024]{1,0:T(8,128)} async-done(((f32[32,1024]{1,0:T(8,128)}), f32[8,1024]{1,0:T(8,128)}) %reduce-scatter.2.cloned.1.call-update) | async-done | bytes 32784 | tf_op jit(solution)/shard_map/reduce_scatter | solution.py:35
  41.5 0.0 copy-done.3
  41.5 0.0 copy-done.2
  41.5 1.6 %fusion.8 = (f32[8]{0:T(128)S(1)}, f32[8,1024]{1,0:T(8,128)S(1)}, bf16[8,1024]{1,0:T(8,128)(2,1)}) fusion(f32[8]{0:T(128)S(1)} %copy-done.2, f32[8,1024]{1,0:T(8,128)} %reduce-scatter.2.cloned.1.call-done, f32[8]{0:T(128)S(1)} %copy-done.3, bf16[1,8,1024]{2,0,1:T(2,128)(2,1)S(1)} %bitcast.17), kind=kLoop, calls=%fused_computation.19 | loop fusion | flops 90104 | bytes 98400 | tf_op jit(solution)/shard_map/reduce_max | solution.py:42
  43.1 11.8 %pmax.7 = f32[8]{0:T(128)S(1)} all-reduce(f32[8]{0:T(128)S(1)} %get-tuple-element.91), channel_id=1, replica_groups=mesh['vocab'=8,'seq'=4] {'vocab'}, use_global_device_ids=true, to_apply=%region_2.3 | all-reduce | flops 8 | bytes 64 | tf_op jit(solution)/shard_map/pmax | solution.py:42
  54.9 0.2 fusion.7
  55.1 11.9 %psum.14 = f32[8]{0:T(128)S(1)} all-reduce(f32[8]{0:T(128)S(1)} %get-tuple-element.89), channel_id=1, replica_groups=mesh['vocab'=8,'seq'=4] {'vocab'}, use_global_device_ids=true, to_apply=%region_4.5 | all-reduce | flops 8 | bytes 64 | tf_op jit(solution)/shard_map/psum | solution.py:44
  66.9 0.0 copy-done.4
  66.9 36.4 %while.13 = (s32[]{:T(128)}, f32[8]{0:T(128)S(1)}, f32[8]{0:T(128)S(1)}, f32[8,1024]{1,0:T(8,128)S(1)}, f32[8]{0:T(128)S(1)}, /*index=5*/f32[8,1024]{1,0:T(8,128)S(1)}, f32[8]{0:T(128)S(1)}, s32[]{:T(128)}, s32[]{:T(128)}) while((s32[]{:T(128)}, f32[8]{0:T(128)S(1)}, f32[8]{0:T(128)S(1)}, f32[8,1024]{1,0:T(8,128)S(1)}, ...), condition=%wide.region_9.10_spmd.clone, body=%wide.region_5.9_spmd.clone.sunk | while | flops 172482 | bytes 67487 | solution.py:61
  67.0 0.1 multiply_subtract_fusion.3
  67.0 0.2 select_reduce_fusion.2
  67.2 11.8 %psum.17 = f32[8,7]{0,1:T(8,128)S(1)} all-reduce(f32[8,7]{0,1:T(8,128)S(1)} %select_reduce_fusion.2), channel_id=1, replica_groups=mesh['vocab'=8,'seq'=4] {'vocab'}, use_global_device_ids=true, to_apply=%region_7.7 | all-reduce | flops 56 | bytes 448 | tf_op jit(solution)/shard_map/while/body/eval_jaxpr/psum | solution.py:56
  79.1 0.1 multiply_subtract_fusion.3
  79.2 0.2 select_reduce_fusion.2
  79.3 11.8 %psum.17 = f32[8,7]{0,1:T(8,128)S(1)} all-reduce(f32[8,7]{0,1:T(8,128)S(1)} %select_reduce_fusion.2), channel_id=1, replica_groups=mesh['vocab'=8,'seq'=4] {'vocab'}, use_global_device_ids=true, to_apply=%region_7.7 | all-reduce | flops 56 | bytes 448 | tf_op jit(solution)/shard_map/while/body/eval_jaxpr/psum | solution.py:56
  91.2 0.1 multiply_subtract_fusion.3
  91.3 0.2 select_reduce_fusion.2
  91.5 11.8 %psum.17 = f32[8,7]{0,1:T(8,128)S(1)} all-reduce(f32[8,7]{0,1:T(8,128)S(1)} %select_reduce_fusion.2), channel_id=1, replica_groups=mesh['vocab'=8,'seq'=4] {'vocab'}, use_global_device_ids=true, to_apply=%region_7.7 | all-reduce | flops 56 | bytes 448 | tf_op jit(solution)/shard_map/while/body/eval_jaxpr/psum | solution.py:56
  103.3 0.5 multiply_subtract_fusion.1
  (17 shorter events, 0.2 us)
Async XLA Ops:
  7.2 15.8 %copy-start = (s32[1,8192]{1,0:T(1,128)S(1)}, s32[1,8192]{1,0:T(1,128)}, u32[]{:S(2)}) copy-start(s32[1,8192]{1,0:T(1,128)} %param.13) | copy-start | bytes 98308
  7.2 15.8 %copy-start.1 = (bf16[1,8192]{1,0:T(2,128)(2,1)S(1)}, bf16[1,8192]{1,0:T(2,128)(2,1)}, u32[]{:S(2)}) copy-start(bf16[1,8192]{1,0:T(2,128)(2,1)} %param.14) | copy-start | bytes 49156
  7.2 34.3 %copy-start.3 = (f32[8]{0:T(128)S(1)}, f32[8]{0:T(128)}, u32[]{:S(2)}) copy-start(f32[8]{0:T(128)} %param.17) | copy-start | bytes 100
  7.2 34.3 %copy-start.2 = (f32[8]{0:T(128)S(1)}, f32[8]{0:T(128)}, u32[]{:S(2)}) copy-start(f32[8]{0:T(128)} %param.18) | copy-start | bytes 100
  7.2 59.7 %copy-start.4 = (f32[8]{0:T(128)S(1)}, f32[8]{0:T(128)}, u32[]{:S(2)}) copy-start(f32[8]{0:T(128)} %param.19) | copy-start | bytes 100
  7.2 34.3 %reduce-scatter.2.cloned.1.call-start = ((), (), s32[]{:S(2)}) async-start(), calls=%async_computation.2 | async-start | bytes 163840 | tf_op jit(solution)/shard_map/reduce_scatter | solution.py:35
  24.9 8.0 %all-to-all-start = ((bf16[8,2,512]{2,1,0:T(2,128)(2,1)}), bf16[8,2,512]{2,1,0:T(2,128)(2,1)S(1)}, u32[]{:S(2)}, u32[]{:S(2)}) async-start(bf16[8,2,512]{2,1,0:T(2,128)(2,1)} %reshape.89), calls=%async_computation | async-start | bytes 32768 | tf_op jit(solution)/shard_map/all_to_all | solution.py:29
Sparse Core Ops, SparseCore 0:
  21.8 19.6 reduce-scatter.1
where the time goes:
time: 111 us
  blocking collectives  70 us (63%)
  between operations  15.4 us (14%)
  waiting for transfers between devices  13.2 us (12%)
  other arithmetic  3.96 us (4%)
  matrix products  3.42 us (3%)
  starting transfers between devices  3.37 us (3%)
  local copies, waits for them, and re-layouts  1.2 us (1%)
    psum x3, blocking collectives, refine(): cumulative_shares = lax.psum(partial_mass, 'vocab')  35.4 us
    psum x1, blocking collectives, per_device(): row_total = lax.psum(jnp.sum(exponential_values, axis=1), 'vocab')  11.9 us
    pmax x1, blocking collectives, per_device(): largest_score = lax.pmax(jnp.max(softened_scores, axis=1), 'vocab')  11.8 us
    all_gather x1, blocking collectives, per_device(): lax.all_gather(latent_vector, 'vocab', axis=0, tiled=True)  10.9 us
    reduce_scatter x1, waiting for transfers between devices, per_device(): lax.psum_scatter(partial_logits, 'seq', scatter_dimension=0, tiled=True)  8.54 us
    all_to_all x1, waiting for transfers between devices, per_device(): lax.all_to_all(offset, 'vocab', split_axis=1, concat_axis=0, tiled=True)  4.67 us
    dot_general x1, matrix products, per_device(): jnp.dot(lax.all_gather(latent_vector, 'vocab', axis=0, tiled=True), unemb...  3.42 us
    all_to_all x1, starting transfers between devices, per_device(): lax.all_to_all(offset, 'vocab', split_axis=1, concat_axis=0, tiled=True)  3.34 us
  transfers between devices with their start and end apart: 2, of which 2 were waited for; matrix products, arithmetic and copies ran while one was open for 2% of the time, Pallas kernels for 0%

commit v1 on v0

v1 whole, which is shorter than its diff:
```python
import jax
import jax.numpy as jnp
from jax import lax
from jax.sharding import PartitionSpec as P

STEPS = 9


cutoff_span = 32.0


def per_device(
    latent_vector,
    unembedding_matrix,
    occurrence_tally,
    additive_offset_table,
    recurrence_charge,
    appearance_charge,
    recurrence_divisor,
    softening_divisor,
    nucleus_share_limit,
):
    vocab_parts = lax.axis_size("vocab")
    seq_parts = lax.axis_size("seq")
    own_rows, vocab = occurrence_tally.shape
    block = unembedding_matrix.shape[1]

    def own(vector):
        return lax.dynamic_slice_in_dim(vector, lax.axis_index("vocab") * own_rows, own_rows, 0)

    factor = own(recurrence_divisor)[:, None]
    softening = own(softening_divisor)[:, None]
    share = own(nucleus_share_limit)

    seen_mask = occurrence_tally > 0
    offset = lax.reduce_precision(
        additive_offset_table.astype(jnp.float32)
        - recurrence_charge[:, None] * occurrence_tally.astype(jnp.float32)
        - appearance_charge[:, None] * seen_mask.astype(jnp.float32),
        exponent_bits=8,
        mantissa_bits=7,
    )

    partial_logits = jnp.dot(
        lax.all_gather(latent_vector, "vocab", axis=0, tiled=True),
        unembedding_matrix,
        preferred_element_type=jnp.float32,
    )
    pieces = partial_logits.reshape(seq_parts * vocab_parts, own_rows, block)
    pieces = lax.all_to_all(pieces, ("seq", "vocab"), split_axis=0, concat_axis=0, tiled=True)
    pieces = pieces.reshape(seq_parts, vocab_parts, own_rows, block).sum(axis=0)
    logits = pieces.transpose(1, 0, 2).reshape(own_rows, vocab)

    discouraged_scores = jnp.where(
        seen_mask, jnp.where(logits > 0, logits / factor, logits * factor), logits
    ) + offset
    softened_scores = discouraged_scores / softening
    largest_score = jnp.max(softened_scores, axis=1)
    exponential_values = jnp.exp(softened_scores - largest_score[:, None])
    target = share * jnp.sum(exponential_values, axis=1)
    lower_end = jnp.zeros_like(largest_score)
    upper_end = jnp.ones_like(largest_score)
    fractions = jnp.arange(1, 8, dtype=jnp.float32)
    for _ in range(STEPS // 3):
        stride = (upper_end - lower_end) * 0.125
        probes = lower_end[:, None] + stride[:, None] * fractions[None, :]
        threshold_candidates = largest_score[:, None] - cutoff_span * probes
        inside = softened_scores[:, None, :] >= threshold_candidates[:, :, None]
        mass = jnp.sum(jnp.where(inside, exponential_values[:, None, :], 0.0), axis=2)
        below_count = jnp.sum((mass < target[:, None]).astype(jnp.float32), axis=1)
        lower_end = lower_end + stride * below_count
        upper_end = lower_end + stride
    cutoff = largest_score - cutoff_span * upper_end

    blocks = discouraged_scores.reshape(own_rows, vocab_parts, block).transpose(1, 0, 2)
    beside = jnp.broadcast_to(cutoff[None, :, None], (vocab_parts, own_rows, 128))
    packed = jnp.concatenate([blocks, beside], axis=2)
    packed = lax.all_to_all(packed, "vocab", split_axis=0, concat_axis=0, tiled=True)
    packed = packed.reshape(vocab_parts * own_rows, block + 128)
    return packed[:, :block].astype(jnp.bfloat16), packed[:, block]


def solution(mesh):
    in_specs = (
        P("vocab", "seq"),
        P("seq", "vocab"),
        P(("seq", "vocab"), None),
        P(("seq", "vocab"), None),
        P(("seq", "vocab")),
        P(("seq", "vocab")),
        P("seq"),
        P("seq"),
        P("seq"),
    )
    out_specs = (P("seq", "vocab"), P("seq"))
    return jax.shard_map(
        per_device, mesh=mesh, in_specs=in_specs, out_specs=out_specs, check_vma=False
    )
```

time: 111 us -> 50.2 us (0.45)
  blocking collectives: 70 us -> 18.3 us
  between operations: 15.4 us -> 5.97 us
  waiting for transfers between devices: 13.2 us -> 5 us
  other arithmetic: 3.96 us -> 8.81 us
  local copies, waits for them, and re-layouts: 1.2 us -> 4.01 us
  starting transfers between devices: 3.37 us -> 4.85 us
    psum x4 -> x0, blocking collectives: 47.3 us -> none  [the longest x3 35.4 us: refine(): cumulative_shares = lax.psum(partial_mass, 'vocab')]
    pmax x1 -> x0, blocking collectives: 11.8 us -> none  [per_device(): largest_score = lax.pmax(jnp.max(softened_scores, axis=1), 'vocab')]
    reduce_scatter x1 -> x0, waiting for transfers between devices: 8.54 us -> none  [per_device(): lax.psum_scatter(partial_logits, 'seq', scatter_dimension=0, tiled=True)]
    all_to_all x0 -> x1, blocking collectives: none -> 7.24 us  [per_device(): lax.all_to_all(packed, 'vocab', split_axis=0, concat_axis=0, tiled=True)]
    reduce_sum x7 -> x8, other arithmetic: 0.78 us -> 4.56 us  [the longest x3 1.86 us: per_device(): below_count = jnp.sum((mass < target[:, None]).astype(jnp.float32), axis=1)]
    dynamic_slice x0 -> x3, local copies, waits for them, and re-layouts: none -> 1.88 us  [own(): lax.dynamic_slice_in_dim(vector, lax.axis_index('vocab') * own_rows, own_...]
    all_to_all x1, starting transfers between devices: 3.34 us -> 4.85 us  [per_device(): lax.all_to_all(pieces, ('seq', 'vocab'), split_axis=0, concat_axis=0, til...]
    sub x4 -> x3, other arithmetic: 0.74 us -> 2.1 us  [per_device(): threshold_candidates = largest_score[:, None] - cutoff_span * probes]
  transfers between devices with their start and end apart: 2 -> 1, of which waited for: 2 -> 1; matrix products, arithmetic and copies ran while one was open for 2% -> 4% of each run, Pallas kernels for 0% -> 0%
where the time goes in v1:
time: 50.2 us; the launch traced here: 49.7 us
  blocking collectives  18.3 us (36%)
  other arithmetic  8.81 us (18%)
  between operations  5.97 us (12%)
  waiting for transfers between devices  5 us (10%)
  starting transfers between devices  4.85 us (10%)
  local copies, waits for them, and re-layouts  4.01 us (8%)
  matrix products  2.77 us (6%)
    all_gather x1, blocking collectives, per_device(): lax.all_gather(latent_vector, 'vocab', axis=0, tiled=True)  11 us
    all_to_all x1, blocking collectives, per_device(): lax.all_to_all(packed, 'vocab', split_axis=0, concat_axis=0, tiled=True)  7.24 us
    all_to_all x1, waiting for transfers between devices, per_device(): lax.all_to_all(pieces, ('seq', 'vocab'), split_axis=0, concat_axis=0, til...  5 us
    all_to_all x1, starting transfers between devices, per_device(): lax.all_to_all(pieces, ('seq', 'vocab'), split_axis=0, concat_axis=0, til...  4.85 us
    dot_general x1, matrix products, per_device(): jnp.dot(lax.all_gather(latent_vector, 'vocab', axis=0, tiled=True), unemb...  2.77 us
    reduce_max x1, other arithmetic, per_device(): largest_score = jnp.max(softened_scores, axis=1)  2.15 us
    sub x3, other arithmetic, per_device(): threshold_candidates = largest_score[:, None] - cutoff_span * probes  2.1 us
    dynamic_slice x3, local copies, waits for them, and re-layouts, own(): lax.dynamic_slice_in_dim(vector, lax.axis_index('vocab') * own_rows, own_...  1.88 us
  transfers between devices with their start and end apart: 1, of which 1 were waited for; matrix products, arithmetic and copies ran while one was open for 4% of the time, Pallas kernels for 0%

profile of v1, /device:TPU:0, one launch (start us, length us, event | category | flops | bytes accessed | tf_op | source)
XLA Modules:
  0.0 49.7 jit_solution(1795570354289927397)
XLA Ops:
  0.6 0.0 copy-start.2
  0.6 0.0 copy-start.3
  0.7 0.0 copy-start.4
  0.7 0.0 copy-start
  0.7 0.0 copy-start.1
  0.7 11.0 %all-gather = bf16[8,4,1792]{2,1,0:T(4,128)(2,1)S(1)} all-gather(bf16[1,4,1792]{2,1,0:T(4,128)(2,1)} %bitcast.43), channel_id=1, replica_groups=mesh['vocab'=8,'seq'=4] {'vocab'}, dimensions={0}, use_global_device_ids=true | all-gather | bytes 129024 | tf_op jit(solution)/shard_map/all_gather | solution.py:45
  11.8 2.8 %convolution_bitcast_fusion = f32[32,1,1024]{2,0,1:T(8,128)S(1)} fusion(bf16[32,1792]{1,0:T(8,128)(2,1)S(1)} %reshape.396, bf16[1792,1024]{1,0:T(8,128)(2,1)} %param.10), kind=kOutput, calls=%fused_computation | convolution fusion | flops 117440512 | bytes 3915776 | tf_op jit(solution)/shard_map/dot_general | solution.py:44
  14.5 0.8 %copy.13 = f32[32,1,1024]{2,1,0:T(1,128)} copy(f32[32,1,1024]{2,0,1:T(8,128)S(1)} %convolution_bitcast_fusion) | data formatting | bytes 262144 | tf_op jit(solution)/shard_map/reshape | solution.py:49
  15.3 4.9 %all-to-all-start = ((f32[32,1,1024]{2,1,0:T(1,128)}), f32[32,1,1024]{2,1,0:T(1,128)S(1)}, u32[]{:S(2)}, u32[]{:S(2)}) async-start(f32[32,1,1024]{2,1,0:T(1,128)} %copy.13), calls=%async_computation | async-start | bytes 262144 | tf_op jit(solution)/shard_map/all_to_all | solution.py:50
  20.2 0.0 copy-done.2
  20.2 0.7 %dynamic_slice.9 = f32[1]{0:T(128)} dynamic-slice(f32[8]{0:T(128)S(1)} %copy-done.2, s32[]{:T(128)S(6)} %select_n.54), dynamic_slice_sizes={1} | dynamic-slice | bytes 12 | tf_op jit(solution)/shard_map/dynamic_slice | solution.py:29
  20.8 0.0 copy-done.3
  20.9 0.6 %dynamic_slice.10 = f32[1]{0:T(128)} dynamic-slice(f32[8]{0:T(128)S(1)} %copy-done.3, s32[]{:T(128)S(6)} %select_n.54), dynamic_slice_sizes={1} | dynamic-slice | bytes 12 | tf_op jit(solution)/shard_map/dynamic_slice | solution.py:29
  22.7 0.0 copy-done.4
  22.7 0.6 %dynamic_slice.11 = f32[1]{0:T(128)} dynamic-slice(f32[8]{0:T(128)S(1)} %copy-done.4, s32[]{:T(128)S(6)} %select_n.54), dynamic_slice_sizes={1} | dynamic-slice | bytes 12 | tf_op jit(solution)/shard_map/dynamic_slice | solution.py:29
  23.4 5.0 %all-to-all-done = f32[32,1,1024]{2,1,0:T(1,128)S(1)} async-done(((f32[32,1,1024]{2,1,0:T(1,128)}), f32[32,1,1024]{2,1,0:T(1,128)S(1)}, u32[]{:S(2)}, u32[]{:S(2)}) %all-to-all-start) | async-done | bytes 131104 | tf_op jit(solution)/shard_map/all_to_all | solution.py:50
  28.4 0.0 copy-done
  28.5 0.0 copy-done.1
  28.5 2.2 %fusion.8 = (f32[]{:T(128)}, f32[1,8192]{1,0:T(1,128)S(1)}, f32[1,8192]{1,0:T(1,128)S(1)}) fusion(f32[]{:T(128)} %bitcast.6, f32[]{:T(128)} %bitcast.31, s32[1,8192]{1,0:T(1,128)S(1)} %copy-done, f32[]{:T(128)} %bitcast.30, bf16[1,8192]{1,0:T(2,128)(2,1)S(1)} %copy-done.1, f32[1,8192]{1,0:T(1,128)S(1)} %bitcast.40, f32[]{:T(128)} %bitcast.2), kind=kLoop, calls=%fused_computation.29 | loop fusion | flops 131071 | bytes 147476 | tf_op jit(solution)/shard_map/reduce_max | solution.py:58
  30.6 0.7 %multiply_subtract_fusion.2 = f32[7]{0:T(128)S(1)} fusion(f32[]{:T(128)} %get-tuple-element.4), kind=kLoop, calls=%fused_computation.26 | loop fusion | flops 21 | bytes 32 | tf_op jit(solution)/shard_map/sub | solution.py:67
  31.3 1.4 %fusion.7 = (f32[]{:T(128)}, f32[1,8192]{1,0:T(1,128)S(1)}) fusion(f32[1,8192]{1,0:T(1,128)S(1)} %get-tuple-element.5, f32[]{:T(128)} %get-tuple-element.4), kind=kLoop, calls=%fused_computation.28 | loop fusion | flops 16383 | bytes 65544 | tf_op jit(solution)/shard_map/reduce_sum | solution.py:60
  34.0 0.4 fusion
  34.4 0.6 %fusion.4 = f32[]{:T(128)} fusion(f32[7]{0:T(128)S(1)} %fusion, f32[]{:T(128)} %bitcast.11), kind=kLoop, calls=%fused_computation.21 | loop fusion | flops 20 | bytes 36 | tf_op jit(solution)/shard_map/reduce_sum | solution.py:70
  35.7 0.7 %multiply_subtract_fusion.1 = f32[7]{0:T(128)S(1)} fusion(f32[]{:T(128)} %bitcast.13, f32[]{:T(128)} %mul_mul.6, f32[]{:T(128)} %get-tuple-element.4), kind=kLoop, calls=%fused_computation.25 | loop fusion | flops 35 | bytes 40 | tf_op jit(solution)/shard_map/sub | solution.py:67
  36.4 0.4 fusion.1
  36.8 0.6 %fusion.5 = f32[]{:T(128)} fusion(f32[7]{0:T(128)S(1)} %fusion.1, f32[]{:T(128)} %bitcast.11), kind=kLoop, calls=%fused_computation.22 | loop fusion | flops 20 | bytes 36 | tf_op jit(solution)/shard_map/reduce_sum | solution.py:70
  38.1 0.7 %multiply_subtract_fusion = f32[7]{0:T(128)S(1)} fusion(f32[]{:T(128)} %bitcast.16, f32[]{:T(128)} %bitcast.15, f32[]{:T(128)} %get-tuple-element.4), kind=kLoop, calls=%fused_computation.24 | loop fusion | flops 35 | bytes 40 | tf_op jit(solution)/shard_map/sub | solution.py:67
  38.8 0.4 fusion.2
  39.2 0.6 %fusion.6 = f32[]{:T(128)} fusion(f32[7]{0:T(128)S(1)} %fusion.2, f32[]{:T(128)} %bitcast.11), kind=kLoop, calls=%fused_computation.23 | loop fusion | flops 20 | bytes 36 | tf_op jit(solution)/shard_map/reduce_sum | solution.py:70
  41.2 7.2 %all_to_all.10 = f32[8,1,1152]{2,1,0:T(1,128)S(1)} all-to-all(f32[8,1,1152]{2,1,0:T(1,128)S(1)} %concatenate.3), channel_id=1, replica_groups=mesh['vocab'=8,'seq'=4] {'vocab'}, dimensions={0} | all-to-all | bytes 73728 | tf_op jit(solution)/shard_map/all_to_all | solution.py:78
  48.5 0.6 %slice.13 = bf16[8,1024]{1,0:T(8,128)(2,1)} slice(f32[8,1152]{1,0:T(8,128)S(1)} %bitcast.41), slice={[0:8], [0:1024]} | slice | bytes 32768 | tf_op jit(solution)/shard_map/slice | solution.py:80
  49.1 0.6 %slice_reduce_fusion = f32[8]{0:T(128)} fusion(f32[8,1152]{1,0:T(8,128)S(1)} %bitcast.42), kind=kLoop, calls=%fused_computation.17 | loop fusion | bytes 64 | tf_op jit(solution)/shard_map/slice | solution.py:80
  (5 shorter events, 0.1 us)
Async XLA Ops:
  0.6 19.6 %copy-start.2 = (f32[8]{0:T(128)S(1)}, f32[8]{0:T(128)}, u32[]{:S(2)}) copy-start(f32[8]{0:T(128)} %param.15) | copy-start | bytes 100
  0.6 20.2 %copy-start.3 = (f32[8]{0:T(128)S(1)}, f32[8]{0:T(128)}, u32[]{:S(2)}) copy-start(f32[8]{0:T(128)} %param.16) | copy-start | bytes 100
  0.7 22.1 %copy-start.4 = (f32[8]{0:T(128)S(1)}, f32[8]{0:T(128)}, u32[]{:S(2)}) copy-start(f32[8]{0:T(128)} %param.17) | copy-start | bytes 100
  0.7 27.8 %copy-start = (s32[1,8192]{1,0:T(1,128)S(1)}, s32[1,8192]{1,0:T(1,128)}, u32[]{:S(2)}) copy-start(s32[1,8192]{1,0:T(1,128)} %param.11) | copy-start | bytes 98308
  0.7 27.8 %copy-start.1 = (bf16[1,8192]{1,0:T(2,128)(2,1)S(1)}, bf16[1,8192]{1,0:T(2,128)(2,1)}, u32[]{:S(2)}) copy-start(bf16[1,8192]{1,0:T(2,128)(2,1)} %param.12) | copy-start | bytes 49156
  15.3 13.1 %all-to-all-start = ((f32[32,1,1024]{2,1,0:T(1,128)}), f32[32,1,1024]{2,1,0:T(1,128)S(1)}, u32[]{:S(2)}, u32[]{:S(2)}) async-start(f32[32,1,1024]{2,1,0:T(1,128)} %copy.13), calls=%async_computation | async-start | bytes 262144 | tf_op jit(solution)/shard_map/all_to_all | solution.py:50
